TPU v7x, 32 devices: a whole 2x2x4 slice. The times are simulated.
32 devices in a mesh: row: 8 (over y, x, core), col: 4 (over z).
Axes of the slice: x: 2, y: 2, z: 4, core: 2. Of those that a mesh axis runs over, the one named last changes fastest.
Arguments:
- query_proj: bfloat16 [192, 192, 128], P('row', 'col'), may hold values from -8 to 8
- key_proj: bfloat16 [192, 192, 128], P('row', 'col'), may hold values from -8 to 8
- value_proj: bfloat16 [192, 192, 128], P('row', 'col'), may hold values from -6 to 6
- pair_bias: bfloat16 [4, 192, 192], P(None, 'col', 'row'), may hold values from -9 to 9
- pair_mask: int32 [192, 192], P('row', 'col'), may hold values 0 or 1
- grad_out: bfloat16 [192, 192, 128], P('row', 'col'), may hold values from -18 to 18
Outputs:
- grad_query: bfloat16 [192, 192, 128], P('row', 'col')
- grad_key: bfloat16 [192, 192, 128], P('row', 'col')
- grad_value: bfloat16 [192, 192, 128], P('row', 'col')
- grad_bias: float32 [4, 192, 192], P(None, 'col', 'row')
All inputs are finite; a program needn't handle non-finite values. No bound on the sum of `pair_mask` on one device may be relied on, other than what follows from the above.
Results may differ from a plain program's by a relative error of at most 0.0096.
Values may be sent and summed in bfloat16 or wider, within the bound.
A program may use at most 128 MiB of HBM per device.

v0:
```python
import functools
import math

import jax
import jax.numpy as jnp
from jax import lax
from jax.experimental import pallas as pl
from jax.experimental.pallas import tpu as pltpu
from jax.sharding import PartitionSpec as P

HEADS = 4
HEAD_DIM = 32


def block_grads(queries, keys_all, values_all, grads, mask_all, bias_full):
    block_rows, query_count, channel_count = queries.shape
    key_count = keys_all.shape[1]
    scale = 1.0 / math.sqrt(HEAD_DIM)
    query_heads = queries.reshape(block_rows, query_count, HEADS, HEAD_DIM)
    key_heads = keys_all.reshape(block_rows, key_count, HEADS, HEAD_DIM)
    value_heads = values_all.reshape(block_rows, key_count, HEADS, HEAD_DIM)
    grad_heads = grads.reshape(block_rows, query_count, HEADS, HEAD_DIM)
    masked = 1000000000.0 * (mask_all.astype(jnp.float32) - 1.0)
    scores = (
        jnp.einsum("bjhd,bkhd->bhjk", query_heads, key_heads, preferred_element_type=jnp.float32)
        * scale
    )
    scores = scores + bias_full.astype(jnp.float32)[None] + masked[:, None, None, :]
    top_score = jnp.max(scores, axis=-1, keepdims=True)
    weights = jnp.exp(scores - top_score)
    attn_probs = weights / jnp.sum(weights, axis=-1, keepdims=True)
    attn_low = attn_probs.astype(jnp.bfloat16)
    attended = jnp.einsum(
        "bhjk,bkhd->bjhd", attn_low, value_heads, preferred_element_type=jnp.float32
    )
    row_delta = jnp.sum(grad_heads.astype(jnp.float32) * attended, axis=-1)
    grad_probs = jnp.einsum(
        "bjhd,bkhd->bhjk", grad_heads, value_heads, preferred_element_type=jnp.float32
    )
    grad_scores = attn_probs * (grad_probs - jnp.transpose(row_delta, (0, 2, 1))[..., None])
    scores_low = grad_scores.astype(jnp.bfloat16)
    grad_queries = (
        jnp.einsum("bhjk,bkhd->bjhd", scores_low, key_heads, preferred_element_type=jnp.float32)
        * scale
    )
    grad_keys = (
        jnp.einsum("bhjk,bjhd->bkhd", scores_low, query_heads, preferred_element_type=jnp.float32)
        * scale
    )
    grad_values = jnp.einsum(
        "bhjk,bjhd->bkhd", attn_low, grad_heads, preferred_element_type=jnp.float32
    )
    bias_grad = jnp.sum(grad_scores, axis=0)
    return (
        grad_queries.reshape(block_rows, query_count, channel_count),
        grad_keys.reshape(block_rows, key_count, channel_count),
        grad_values.reshape(block_rows, key_count, channel_count),
        bias_grad,
    )


def all_blocks(queries, keys_all, values_all, grads, mask_all, bias_full):
    row_count, query_count, channel_count = queries.shape
    key_count = keys_all.shape[1]
    block_rows = 1
    while (
        block_rows * 2 <= row_count
        and row_count % (block_rows * 2) == 0
        and (block_rows * query_count < 512)
    ):
        block_rows = block_rows * 2
    steps_count = row_count // block_rows

    def split_rows(array):
        return array.reshape((steps_count, block_rows) + array.shape[1:])

    def one_block(bias_sum, pieces):
        grad_queries, grad_keys, grad_values, bias_grad = block_grads(
            pieces[0], pieces[1], pieces[2], pieces[3], pieces[4], bias_full
        )
        return (bias_sum + bias_grad, (grad_queries, grad_keys, grad_values))

    start_sum = jnp.zeros((HEADS, query_count, key_count), jnp.float32)
    bias_sum, stacked = lax.scan(
        one_block,
        start_sum,
        (
            split_rows(queries),
            split_rows(keys_all),
            split_rows(values_all),
            split_rows(grads),
            split_rows(mask_all),
        ),
    )
    return (
        stacked[0].reshape(row_count, query_count, channel_count),
        stacked[1].reshape(row_count, key_count, channel_count),
        stacked[2].reshape(row_count, key_count, channel_count),
        bias_sum,
    )


def local(query_proj, key_proj, value_proj, pair_bias, pair_mask, grad_out):
    bias_rows = lax.all_gather(pair_bias, "row", axis=2, tiled=True)
    mask_low = pair_mask.astype(jnp.bfloat16)
    local_tiles = (
        lax.all_to_all(query_proj, "col", split_axis=0, concat_axis=1, tiled=True),
        lax.all_to_all(key_proj, "col", split_axis=0, concat_axis=1, tiled=True),
        lax.all_to_all(value_proj, "col", split_axis=0, concat_axis=1, tiled=True),
        lax.all_to_all(grad_out, "col", split_axis=0, concat_axis=1, tiled=True),
        lax.all_to_all(mask_low, "col", split_axis=0, concat_axis=1, tiled=True),
    )
    bias_full = lax.all_gather(bias_rows, "col", axis=1, tiled=True)
    grad_queries, grad_keys, grad_values, bias_whole = all_blocks(
        local_tiles[0], local_tiles[1], local_tiles[2], local_tiles[3], local_tiles[4], bias_full
    )
    grad_query, grad_key, grad_value = (
        lax.all_to_all(
            grad_queries.astype(jnp.bfloat16), "col", split_axis=1, concat_axis=0, tiled=True
        ),
        lax.all_to_all(
            grad_keys.astype(jnp.bfloat16), "col", split_axis=1, concat_axis=0, tiled=True
        ),
        lax.all_to_all(
            grad_values.astype(jnp.bfloat16), "col", split_axis=1, concat_axis=0, tiled=True
        ),
    )
    bias_part = lax.psum_scatter(bias_whole, "col", scatter_dimension=1, tiled=True)
    grad_bias = lax.psum_scatter(bias_part, "row", scatter_dimension=2, tiled=True)
    return (grad_query, grad_key, grad_value, grad_bias)


HELD_CHUNKS = 0
MESH = pl.DeviceIdType.MESH


def round_up(value, step):
    return -(-value // step) * step


def fused_kernel(
    rows_n, cols_n, pack,
    q_ref, k_ref, v_ref, g_ref, bias_in, mask_in,
    gq_ref, gk_ref, gv_ref, gb_ref,
    bias_ref, mask_ref, got, stage, bias_all, mask_all, bias_full, bias_sum, part, part_in, tile, tile_in,
    in_send, in_recv, out_send, out_recv, bc_send, bc_recv, br_send, br_recv,
    mk_send, mk_recv, pr_send, pr_recv, pc_send, pc_recv, own_sem,
):
    row, col = lax.axis_index("row"), lax.axis_index("col")
    per = got.shape[1]
    count = got.shape[2]
    width = q_ref.shape[1]
    keys = bias_sum.shape[1] // rows_n
    rows_here = mask_in.shape[0]
    packs, padded, lanes = bias_ref.shape
    chunk = 2 if per % 2 == 0 else 1
    chunks = per // chunk
    held = min(chunks, HELD_CHUNKS)
    scale = 1.0 / math.sqrt(HEAD_DIM)
    sources = (q_ref, k_ref, v_ref, g_ref)
    results = (gq_ref, gk_ref, gv_ref)

    def row_peer(d):
        return (lax.rem(row + d, rows_n), col)

    paired = cols_n & (cols_n - 1) == 0

    def col_peer(d):
        if not paired:
            return (row, lax.rem(col + d, cols_n))
        other = 0
        bit = 1
        while bit < cols_n:
            mine = lax.rem(col // bit, 2)
            other = other + bit * (1 - mine if d & bit else mine)
            bit = bit * 2
        return (row, other)

    def remote(src, dst, send, recv, peer):
        return pltpu.make_async_remote_copy(
            src_ref=src, dst_ref=dst, send_sem=send, recv_sem=recv,
            device_id=peer, device_id_type=MESH,
        )

    nn = (((1,), (0,)), ((), ()))
    nt = (((1,), (1,)), ((), ()))
    tn = (((0,), (0,)), ((), ()))
    barrier = pltpu.get_barrier_semaphore()
    for d in range(1, rows_n):
        pl.semaphore_signal(barrier, inc=1, device_id=row_peer(d), device_id_type=MESH)
    for d in range(1, cols_n):
        pl.semaphore_signal(barrier, inc=1, device_id=col_peer(d), device_id_type=MESH)

    def shifted(shape, shift):
        at = lax.broadcasted_iota(jnp.int32, shape, 0)
        lane = lax.broadcasted_iota(jnp.int32, shape, 1)
        return jnp.where(lane == at + shift, 1.0, 0.0).astype(jnp.bfloat16)

    bias_ref[...] = jnp.zeros_like(bias_ref)
    for p in range(packs):
        flipped = jnp.zeros((keys, lanes), jnp.float32)
        for hh in range(pack):
            flipped = flipped + lax.dot_general(
                bias_in[p * pack + hh], shifted((width, lanes), hh * width), nn,
                preferred_element_type=jnp.float32,
            )
        bias_ref[p, 0:keys, :] = flipped.astype(jnp.bfloat16)
    mask_ref[...] = lax.dot_general(
        mask_in[...].astype(jnp.float32).astype(jnp.bfloat16),
        shifted((rows_here, mask_ref.shape[1]), 0), tn,
        preferred_element_type=jnp.float32,
    ).astype(jnp.bfloat16)
    pl.semaphore_wait(barrier, rows_n + cols_n - 2)

    my_cols = pl.ds(pl.multiple_of(col * width, width), width)
    bias_col = [
        remote(bias_ref, bias_all.at[row, col], bc_send.at[d], bc_recv.at[d], col_peer(d))
        for d in range(1, cols_n)
    ]
    mask_col = [
        remote(mask_ref, mask_all.at[my_cols], mk_send.at[d], mk_recv.at[d], col_peer(d))
        for d in range(1, cols_n)
    ]
    for copy in bias_col + mask_col:
        copy.start()
    own = [
        pltpu.make_async_copy(bias_ref, bias_all.at[row, col], own_sem.at[0]),
        pltpu.make_async_copy(mask_ref, mask_all.at[my_cols], own_sem.at[1]),
    ]
    for a in range(4):
        own.append(pltpu.make_async_copy(
            sources[a].at[pl.ds(col * per, per)], got.at[a, :, my_cols], own_sem.at[2 + a]
        ))
    for copy in own:
        copy.start()

    def in_copies(c):
        copies = []
        for d in reversed(range(1, cols_n)):
            peer = col_peer(d)
            for a in range(4):
                copies.append(remote(
                    sources[a].at[pl.ds(peer[1] * per + c * chunk, chunk)],
                    got.at[a, pl.ds(c * chunk, chunk), my_cols],
                    in_send.at[c, d, a], in_recv.at[c, d, a], peer,
                ))
        return copies

    def out_copies(c):
        copies = []
        for d in reversed(range(1, cols_n)):
            peer = col_peer(d)
            there = pl.ds(pl.multiple_of(peer[1] * width, width), width)
            for a in range(3):
                copies.append(remote(
                    stage.at[a, pl.ds(c * chunk, chunk), there],
                    results[a].at[pl.ds(col * per + c * chunk, chunk)],
                    out_send.at[c, d, a], out_recv.at[c, d, a], peer,
                ))
        return copies

    def own_outs(c):
        return [
            pltpu.make_async_copy(
                stage.at[a, pl.ds(c * chunk, chunk), my_cols],
                results[a].at[pl.ds(col * per + c * chunk, chunk)],
                out_send.at[c, 0, a],
            )
            for a in range(3)
        ]

    @pl.loop(0, chunks)
    def _(c):
        for copy in in_copies(c):
            copy.start()

    for copy in bias_col:
        copy.wait_recv()
    for copy in own:
        copy.wait()
    bias_row = [
        remote(bias_all.at[row], bias_all.at[row], br_send.at[d], br_recv.at[d], row_peer(d))
        for d in range(1, rows_n)
    ]
    for copy in bias_row:
        copy.start()
    bias_sum[...] = jnp.zeros_like(bias_sum)
    part[...] = jnp.zeros_like(part)
    for copy in mask_col:
        copy.wait_recv()
    for copy in bias_row:
        copy.wait_recv()

    def pick(z, hh, shape, lane_axis):
        lane = lax.broadcasted_iota(jnp.int32, shape, lane_axis)
        at = lax.broadcasted_iota(jnp.int32, shape, 1 - lane_axis)
        inside = (lane >= hh * width) & (lane < (hh + 1) * width)
        return jnp.where(inside & (lane + (z - hh) * width == at), 1.0, 0.0).astype(jnp.bfloat16)

    for p in range(packs):
        for hh in range(pack):
            whole = jnp.zeros((rows_n * padded, count), jnp.float32)
            for z in range(cols_n):
                piece = bias_all[:, z, p].reshape(rows_n * padded, lanes)
                whole = whole + jnp.dot(
                    piece, pick(z, hh, (lanes, count), 0), preferred_element_type=jnp.float32
                )
            for r in range(rows_n):
                bias_full[p * pack + hh, r * keys:(r + 1) * keys, :] = (
                    whole[r * padded:r * padded + keys]
                )

    channel = lax.broadcasted_iota(jnp.int32, (count, HEADS * HEAD_DIM), 1)
    mask_lane = lax.broadcasted_iota(jnp.int32, mask_all.shape, 1)

    def one_row(i):
        q, k, v, g = got[0, i], got[1, i], got[2, i], got[3, i]
        present = jnp.sum(
            jnp.where(mask_lane == col * per + i, mask_all[...].astype(jnp.float32), 0.0),
            axis=1, keepdims=True,
        )
        masked = 1000000000.0 * (present - 1.0)
        gq = jnp.zeros((count, HEADS * HEAD_DIM), jnp.float32)
        gk = gq
        gv = gq
        for h in range(HEADS):
            mine = (channel >= h * HEAD_DIM) & (channel < (h + 1) * HEAD_DIM)

            def only(x):
                return jnp.where(mine, x, jnp.zeros_like(x))

            kh, vh, qh, gh = only(k), only(v), only(q), only(g)
            scores = lax.dot_general(kh, q, nt, preferred_element_type=jnp.float32) * scale
            scores = scores + bias_full[h] + masked
            weights = jnp.exp(scores - jnp.max(scores, axis=0, keepdims=True))
            probs = weights * (1.0 / jnp.sum(weights, axis=0, keepdims=True))
            low = probs.astype(jnp.bfloat16)
            grad_probs = lax.dot_general(vh, g, nt, preferred_element_type=jnp.float32)
            delta = jnp.sum(low.astype(jnp.float32) * grad_probs, axis=0, keepdims=True)
            grad_scores = probs * (grad_probs - delta)
            bias_sum[h] += grad_scores
            slow = grad_scores.astype(jnp.bfloat16)
            gq = gq + lax.dot_general(slow, kh, tn, preferred_element_type=jnp.float32)
            gk = gk + jnp.dot(slow, qh, preferred_element_type=jnp.float32)
            gv = gv + jnp.dot(low, gh, preferred_element_type=jnp.float32)
        stage[0, i] = (gq * scale).astype(jnp.bfloat16)
        stage[1, i] = (gk * scale).astype(jnp.bfloat16)
        stage[2, i] = gv.astype(jnp.bfloat16)

    @pl.loop(0, chunks)
    def _(c):
        for copy in in_copies(c):
            copy.wait_recv()

        @pl.loop(0, chunk)
        def _(r):
            one_row(c * chunk + r)

        for copy in own_outs(c):
            copy.start()

        @pl.when(c < chunks - held)
        def _():
            for copy in out_copies(c):
                copy.start()

    for r in range(rows_n):
        for h in range(HEADS):
            part[r, h, 0:keys, :] = bias_sum[h, r * keys:(r + 1) * keys, :].astype(jnp.bfloat16)
    part_row = []
    for d in range(1, rows_n):
        peer = row_peer(d)
        part_row.append(remote(
            part.at[peer[0]], part_in.at[row], pr_send.at[d], pr_recv.at[d], peer
        ))
    for copy in part_row:
        copy.start()
    for copy in part_row:
        copy.wait_recv()
    sums = []
    for h in range(HEADS):
        total = part[row, h].astype(jnp.float32)
        for d in range(1, rows_n):
            total = total + part_in[lax.rem(row + d, rows_n), h].astype(jnp.float32)
        sums.append(total.astype(jnp.bfloat16))
    for z in range(cols_n):
        for p in range(packs):
            packed = jnp.zeros((padded, lanes), jnp.float32)
            for hh in range(pack):
                packed = packed + jnp.dot(
                    sums[p * pack + hh], pick(z, hh, (count, lanes), 1),
                    preferred_element_type=jnp.float32,
                )
            tile[z, p] = packed.astype(jnp.bfloat16)
    part_col = []
    for d in range(1, cols_n):
        peer = col_peer(d)
        part_col.append(remote(
            tile.at[peer[1]], tile_in.at[col], pc_send.at[d], pc_recv.at[d], peer
        ))
    for copy in part_col:
        copy.start()

    @pl.loop(chunks - held, chunks)
    def _(c):
        for copy in out_copies(c):
            copy.start()

    for copy in part_col:
        copy.wait_recv()
    total = tile[col].astype(jnp.float32)
    for d in range(1, cols_n):
        total = total + tile_in[lax.rem(col + d, cols_n)].astype(jnp.float32)
    for p in range(packs):
        for hh in range(pack):
            gb_ref[p * pack + hh] = total[p, 0:keys, hh * width:(hh + 1) * width]

    @pl.loop(0, chunks)
    def _(c):
        for copy in in_copies(c):
            copy.wait_send()
        for copy in out_copies(c):
            copy.wait()
        for copy in own_outs(c):
            copy.wait()

    for copy in bias_col + mask_col + bias_row + part_row + part_col:
        copy.wait_send()


def fused(rows_n, cols_n, query_proj, key_proj, value_proj, pair_bias, pair_mask, grad_out):
    rows, width, channels = query_proj.shape
    keys = pair_bias.shape[2]
    per, count = rows // cols_n, width * cols_n
    pack = 1
    while pack * 2 <= HEADS and pack * 2 * width <= 128:
        pack = pack * 2
    packs = HEADS // pack
    padded, lanes = round_up(keys, 16), round_up(pack * width, 128)
    mask_lanes = round_up(rows, 128)
    chunk = 2 if per % 2 == 0 else 1
    chunks = per // chunk
    bf16, f32 = jnp.bfloat16, jnp.float32
    anywhere = pl.BlockSpec(memory_space=pl.ANY)
    on_chip = pl.BlockSpec(memory_space=pltpu.VMEM)
    sem = pltpu.SemaphoreType.DMA
    tile_shape = pltpu.VMEM(query_proj.shape, bf16)
    gq, gk, gv, gb = pl.pallas_call(
        functools.partial(fused_kernel, rows_n, cols_n, pack),
        name="triangle_grads",
        out_shape=(
            tile_shape, tile_shape, tile_shape,
            jax.ShapeDtypeStruct((HEADS, keys, width), f32),
        ),
        in_specs=[anywhere] * 4 + [on_chip] * 2,
        out_specs=(on_chip,) * 4,
        scratch_shapes=[
            pltpu.VMEM((packs, padded, lanes), bf16),
            pltpu.VMEM((width, mask_lanes), bf16),
            pltpu.VMEM((4, per, count, channels), bf16),
            pltpu.VMEM((3, per, count, channels), bf16),
            pltpu.VMEM((rows_n, cols_n, packs, padded, lanes), bf16),
            pltpu.VMEM((count, mask_lanes), bf16),
            pltpu.VMEM((HEADS, count, count), f32),
            pltpu.VMEM((HEADS, count, count), f32),
            pltpu.VMEM((rows_n, HEADS, padded, count), bf16),
            pltpu.VMEM((rows_n, HEADS, padded, count), bf16),
            pltpu.VMEM((cols_n, packs, padded, lanes), bf16),
            pltpu.VMEM((cols_n, packs, padded, lanes), bf16),
            sem((chunks, cols_n, 4)), sem((chunks, cols_n, 4)),
            sem((chunks, cols_n, 3)), sem((chunks, cols_n, 3)),
            sem((cols_n,)), sem((cols_n,)),
            sem((rows_n,)), sem((rows_n,)),
            sem((cols_n,)), sem((cols_n,)),
            sem((rows_n,)), sem((rows_n,)),
            sem((cols_n,)), sem((cols_n,)),
            sem((6,)),
        ],
        compiler_params=pltpu.CompilerParams(collective_id=0, has_side_effects=True),
    )(query_proj, key_proj, value_proj, grad_out, jnp.transpose(pair_bias, (0, 2, 1)), pair_mask)
    return gq, gk, gv, jnp.transpose(gb, (0, 2, 1))


def choose(rows_n, cols_n):
    def run(*arrays):
        count = arrays[0].shape[1] * cols_n
        if count * count * 4 <= 512 * 1024 and arrays[0].shape[0] % cols_n == 0:
            return fused(rows_n, cols_n, *arrays)
        return local(*arrays)

    return run


def solution(mesh):
    placed = (
        P("row", "col", None),
        P("row", "col", None),
        P("row", "col", None),
        P(None, "col", "row"),
        P("row", "col"),
        P("row", "col", None),
    )
    return jax.shard_map(
        choose(mesh.shape["row"], mesh.shape["col"]),
        mesh=mesh,
        in_specs=placed,
        out_specs=(
            P("row", "col", None),
            P("row", "col", None),
            P("row", "col", None),
            P(None, "col", "row"),
        ),
        check_vma=False,
    )
```

profile of v0, /device:TPU:0, one launch (start us, length us, event | category | flops | bytes accessed | tf_op | source)
XLA Modules:
  0.0 62.6 jit_solution(4399110090271117301)
XLA Ops:
  0.6 59.1 %triangle_grads.1 = (bf16[24,48,128]{2,1,0:T(8,128)(2,1)S(1)}, bf16[24,48,128]{2,1,0:T(8,128)(2,1)S(1)}, bf16[24,48,128]{2,1,0:T(8,128)(2,1)S(1)}, f32[4,24,48]{2,1,0:T(8,128)}) custom-call(bf16[24,48,128]{2,1,0:T(8,128)(2,1)} %q_ref.1, bf16[24,48,128]{2,1,0:T(8,128)(2,1)} %k_ref.1, bf16[24,48,128]{2,1,0:T(8,128)(2,1)} %v_ref.1, bf16[24,48,128]{2,1,0:T(8,128)(2,1)} %g_ref.1, ...), custom_call_target="tpu_custom_call" | custom-call | tf_op jit(solution)/shard_map/triangle_grads/pallas_call | solution.py:448
  59.7 0.7 %copy.14 = bf16[24,48,128]{2,1,0:T(8,128)(2,1)} copy(bf16[24,48,128]{2,1,0:T(8,128)(2,1)S(1)} %get-tuple-element.12) | data formatting | bytes 589824
  60.5 0.7 %copy.15 = bf16[24,48,128]{2,1,0:T(8,128)(2,1)} copy(bf16[24,48,128]{2,1,0:T(8,128)(2,1)S(1)} %get-tuple-element.13) | data formatting | bytes 589824
  61.2 0.0 copy-start
  61.2 0.7 %copy.16 = bf16[24,48,128]{2,1,0:T(8,128)(2,1)} copy(bf16[24,48,128]{2,1,0:T(8,128)(2,1)S(1)} %get-tuple-element.14) | data formatting | bytes 589824
  61.9 0.1 copy-done
  62.0 0.6 copy.17
Async XLA Ops:
  61.2 0.8 %copy-start = (f32[4,24,48]{2,1,0:T(8,128)S(1)}, f32[4,24,48]{2,1,0:T(8,128)}, u32[]{:S(2)}) copy-start(f32[4,24,48]{2,1,0:T(8,128)} %get-tuple-element.11) | copy-start | bytes 55300
where the time goes:
time: 62.8 us; the launch traced here: 62.6 us
  Pallas kernels  59.1 us (94%)
  local copies, waits for them, and re-layouts  2.85 us (5%)
  between operations  0.64 us (1%)
    pallas_call x1, Pallas kernels, fused(): pl.pallas_call(functools.partial(fused_kernel, rows_n, cols_n, pack), nam...  59.1 us
    unnamed x6, local copies, waits for them, and re-layouts  2.85 us

commit v1 on v0

--- a/solution.py
+++ b/solution.py
@@ -130,7 +130,6 @@
     return (grad_query, grad_key, grad_value, grad_bias)
 
 
-HELD_CHUNKS = 0
 MESH = pl.DeviceIdType.MESH
 
 
@@ -142,9 +141,8 @@
     rows_n, cols_n, pack,
     q_ref, k_ref, v_ref, g_ref, bias_in, mask_in,
     gq_ref, gk_ref, gv_ref, gb_ref,
-    bias_ref, mask_ref, got, stage, bias_all, mask_all, bias_full, bias_sum, part, part_in, tile, tile_in,
-    in_send, in_recv, out_send, out_recv, bc_send, bc_recv, br_send, br_recv,
-    mk_send, mk_recv, pr_send, pr_recv, pc_send, pc_recv, own_sem,
+    bias_send, got, stage, bias_all, mask_all, bias_full, bias_sum, part, part_in, tile, tile_in,
+    in_recv, sems, own_sem,
 ):
     row, col = lax.axis_index("row"), lax.axis_index("col")
     per = got.shape[1]
@@ -152,13 +150,16 @@
     width = q_ref.shape[1]
     keys = bias_sum.shape[1] // rows_n
     rows_here = mask_in.shape[0]
-    packs, padded, lanes = bias_ref.shape
+    _, packs, padded, lanes = bias_send.shape
     chunk = 2 if per % 2 == 0 else 1
     chunks = per // chunk
-    held = min(chunks, HELD_CHUNKS)
     scale = 1.0 / math.sqrt(HEAD_DIM)
     sources = (q_ref, k_ref, v_ref, g_ref)
     results = (gq_ref, gk_ref, gv_ref)
+    others = (cols_n - 1) * width
+    in_send, out_send, out_recv, bc_send, bc_recv, br_send, br_recv, pr_send, pr_recv, pc_send, pc_recv = (
+        sems.at[n] for n in range(11)
+    )
 
     def row_peer(d):
         return (lax.rem(row + d, rows_n), col)
@@ -186,17 +187,23 @@
     nt = (((1,), (1,)), ((), ()))
     tn = (((0,), (0,)), ((), ()))
     barrier = pltpu.get_barrier_semaphore()
+    for d in range(1, cols_n):
+        pl.semaphore_signal(barrier, inc=1, device_id=col_peer(d), device_id_type=MESH)
     for d in range(1, rows_n):
         pl.semaphore_signal(barrier, inc=1, device_id=row_peer(d), device_id_type=MESH)
-    for d in range(1, cols_n):
-        pl.semaphore_signal(barrier, inc=1, device_id=col_peer(d), device_id_type=MESH)
+    my_cols = pl.ds(pl.multiple_of(col * width, width), width)
+    for a in range(4):
+        pltpu.make_async_copy(
+            sources[a].at[pl.ds(col * per, per)], got.at[a, :, my_cols], own_sem
+        ).start()
 
     def shifted(shape, shift):
         at = lax.broadcasted_iota(jnp.int32, shape, 0)
         lane = lax.broadcasted_iota(jnp.int32, shape, 1)
         return jnp.where(lane == at + shift, 1.0, 0.0).astype(jnp.bfloat16)
 
-    bias_ref[...] = jnp.zeros_like(bias_ref)
+    mask_low = mask_in[...].astype(jnp.float32).astype(jnp.bfloat16)
+    bases = []
     for p in range(packs):
         flipped = jnp.zeros((keys, lanes), jnp.float32)
         for hh in range(pack):
@@ -204,92 +211,69 @@
                 bias_in[p * pack + hh], shifted((width, lanes), hh * width), nn,
                 preferred_element_type=jnp.float32,
             )
-        bias_ref[p, 0:keys, :] = flipped.astype(jnp.bfloat16)
-    mask_ref[...] = lax.dot_general(
-        mask_in[...].astype(jnp.float32).astype(jnp.bfloat16),
-        shifted((rows_here, mask_ref.shape[1]), 0), tn,
-        preferred_element_type=jnp.float32,
+        bases.append(flipped.astype(jnp.bfloat16))
+    wide_mask = lax.dot_general(
+        mask_low, shifted((width, lanes), 0), nn, preferred_element_type=jnp.float32
     ).astype(jnp.bfloat16)
+    for z in range(cols_n):
+        for p in range(packs):
+            bias_send[z, p, 0:keys, :] = bases[p]
+        at = lax.broadcasted_iota(jnp.int32, (padded - keys, rows_here), 0)
+        pos = lax.broadcasted_iota(jnp.int32, (padded - keys, rows_here), 1)
+        pick_rows = jnp.where((pos == at + z * per) & (at < per), 1.0, 0.0).astype(jnp.bfloat16)
+        piece = jnp.dot(pick_rows, wide_mask, preferred_element_type=jnp.float32)
+        bias_send[z, 0, keys:padded, :] = piece.astype(jnp.bfloat16)
+        for p in range(1, packs):
+            bias_send[z, p, keys:padded, :] = jnp.zeros((padded - keys, lanes), jnp.bfloat16)
+    bias_all[row, col] = bias_send[col]
     pl.semaphore_wait(barrier, rows_n + cols_n - 2)
 
-    my_cols = pl.ds(pl.multiple_of(col * width, width), width)
-    bias_col = [
-        remote(bias_ref, bias_all.at[row, col], bc_send.at[d], bc_recv.at[d], col_peer(d))
-        for d in range(1, cols_n)
-    ]
-    mask_col = [
-        remote(mask_ref, mask_all.at[my_cols], mk_send.at[d], mk_recv.at[d], col_peer(d))
-        for d in range(1, cols_n)
-    ]
-    for copy in bias_col + mask_col:
-        copy.start()
-    own = [
-        pltpu.make_async_copy(bias_ref, bias_all.at[row, col], own_sem.at[0]),
-        pltpu.make_async_copy(mask_ref, mask_all.at[my_cols], own_sem.at[1]),
-    ]
-    for a in range(4):
-        own.append(pltpu.make_async_copy(
-            sources[a].at[pl.ds(col * per, per)], got.at[a, :, my_cols], own_sem.at[2 + a]
-        ))
-    for copy in own:
-        copy.start()
-
-    def in_copies(c):
-        copies = []
+    for d in range(1, cols_n):
+        peer = col_peer(d)
+        remote(bias_send.at[peer[1]], bias_all.at[row, col], bc_send, bc_recv, peer).start()
+
+    @pl.loop(0, chunks)
+    def _(c):
         for d in reversed(range(1, cols_n)):
             peer = col_peer(d)
             for a in range(4):
-                copies.append(remote(
+                remote(
                     sources[a].at[pl.ds(peer[1] * per + c * chunk, chunk)],
                     got.at[a, pl.ds(c * chunk, chunk), my_cols],
-                    in_send.at[c, d, a], in_recv.at[c, d, a], peer,
-                ))
-        return copies
-
-    def out_copies(c):
-        copies = []
+                    in_send, in_recv.at[c], peer,
+                ).start()
+
+    def out_start(c):
         for d in reversed(range(1, cols_n)):
             peer = col_peer(d)
             there = pl.ds(pl.multiple_of(peer[1] * width, width), width)
             for a in range(3):
-                copies.append(remote(
+                remote(
                     stage.at[a, pl.ds(c * chunk, chunk), there],
                     results[a].at[pl.ds(col * per + c * chunk, chunk)],
-                    out_send.at[c, d, a], out_recv.at[c, d, a], peer,
-                ))
-        return copies
-
-    def own_outs(c):
-        return [
-            pltpu.make_async_copy(
-                stage.at[a, pl.ds(c * chunk, chunk), my_cols],
-                results[a].at[pl.ds(col * per + c * chunk, chunk)],
-                out_send.at[c, 0, a],
-            )
-            for a in range(3)
-        ]
-
-    @pl.loop(0, chunks)
-    def _(c):
-        for copy in in_copies(c):
-            copy.start()
-
-    for copy in bias_col:
-        copy.wait_recv()
-    for copy in own:
-        copy.wait()
-    bias_row = [
-        remote(bias_all.at[row], bias_all.at[row], br_send.at[d], br_recv.at[d], row_peer(d))
-        for d in range(1, rows_n)
-    ]
-    for copy in bias_row:
-        copy.start()
+                    out_send, out_recv, peer,
+                ).start()
+
     bias_sum[...] = jnp.zeros_like(bias_sum)
     part[...] = jnp.zeros_like(part)
-    for copy in mask_col:
-        copy.wait_recv()
-    for copy in bias_row:
-        copy.wait_recv()
+    near = col_peer(1)
+    side = row_peer(1)
+    first = bias_all.at[0, 0:cols_n - 1]
+    remote(first, first, bc_send, bc_recv, near).wait_recv()
+    for d in range(1, rows_n):
+        remote(bias_all.at[row], bias_all.at[row], br_send, br_recv, row_peer(d)).start()
+    mask_sum = jnp.zeros((count, padded - keys), jnp.float32)
+    for z in range(cols_n):
+        at = lax.broadcasted_iota(jnp.int32, (count, lanes), 0)
+        lane = lax.broadcasted_iota(jnp.int32, (count, lanes), 1)
+        lift = jnp.where((lane < width) & (at == lane + z * width), 1.0, 0.0).astype(jnp.bfloat16)
+        mask_sum = mask_sum + lax.dot_general(
+            lift, bias_all[row, z, 0, keys:padded, :], nt, preferred_element_type=jnp.float32
+        )
+    mask_all[...] = mask_sum
+    pltpu.make_async_copy(got.at[:, :, my_cols], got.at[:, :, my_cols], own_sem).wait()
+    most = bias_all.at[0:rows_n - 1]
+    remote(most, most, br_send, br_recv, side).wait_recv()
 
     def pick(z, hh, shape, lane_axis):
         lane = lax.broadcasted_iota(jnp.int32, shape, lane_axis)
@@ -316,8 +300,7 @@
     def one_row(i):
         q, k, v, g = got[0, i], got[1, i], got[2, i], got[3, i]
         present = jnp.sum(
-            jnp.where(mask_lane == col * per + i, mask_all[...].astype(jnp.float32), 0.0),
-            axis=1, keepdims=True,
+            jnp.where(mask_lane == i, mask_all[...], 0.0), axis=1, keepdims=True,
         )
         masked = 1000000000.0 * (present - 1.0)
         gq = jnp.zeros((count, HEADS * HEAD_DIM), jnp.float32)
@@ -349,34 +332,27 @@
 
     @pl.loop(0, chunks)
     def _(c):
-        for copy in in_copies(c):
-            copy.wait_recv()
+        landed = got.at[:, pl.ds(c * chunk, chunk), 0:others]
+        remote(landed, landed, in_send, in_recv.at[c], near).wait_recv()
 
         @pl.loop(0, chunk)
         def _(r):
             one_row(c * chunk + r)
 
-        for copy in own_outs(c):
-            copy.start()
-
-        @pl.when(c < chunks - held)
-        def _():
-            for copy in out_copies(c):
-                copy.start()
+        out_start(c)
+        for a in range(3):
+            results[a][pl.ds(col * per + c * chunk, chunk)] = (
+                stage[a, pl.ds(c * chunk, chunk), my_cols]
+            )
 
     for r in range(rows_n):
         for h in range(HEADS):
             part[r, h, 0:keys, :] = bias_sum[h, r * keys:(r + 1) * keys, :].astype(jnp.bfloat16)
-    part_row = []
     for d in range(1, rows_n):
         peer = row_peer(d)
-        part_row.append(remote(
-            part.at[peer[0]], part_in.at[row], pr_send.at[d], pr_recv.at[d], peer
-        ))
-    for copy in part_row:
-        copy.start()
-    for copy in part_row:
-        copy.wait_recv()
+        remote(part.at[peer[0]], part_in.at[row], pr_send, pr_recv, peer).start()
+    many = part_in.at[0:rows_n - 1]
+    remote(many, many, pr_send, pr_recv, side).wait_recv()
     sums = []
     for h in range(HEADS):
         total = part[row, h].astype(jnp.float32)
@@ -392,22 +368,11 @@
                     preferred_element_type=jnp.float32,
                 )
             tile[z, p] = packed.astype(jnp.bfloat16)
-    part_col = []
     for d in range(1, cols_n):
         peer = col_peer(d)
-        part_col.append(remote(
-            tile.at[peer[1]], tile_in.at[col], pc_send.at[d], pc_recv.at[d], peer
-        ))
-    for copy in part_col:
-        copy.start()
-
-    @pl.loop(chunks - held, chunks)
-    def _(c):
-        for copy in out_copies(c):
-            copy.start()
-
-    for copy in part_col:
-        copy.wait_recv()
+        remote(tile.at[peer[1]], tile_in.at[col], pc_send, pc_recv, peer).start()
+    few = tile_in.at[0:cols_n - 1]
+    remote(few, few, pc_send, pc_recv, near).wait_recv()
     total = tile[col].astype(jnp.float32)
     for d in range(1, cols_n):
         total = total + tile_in[lax.rem(col + d, cols_n)].astype(jnp.float32)
@@ -415,17 +380,37 @@
         for hh in range(pack):
             gb_ref[p * pack + hh] = total[p, 0:keys, hh * width:(hh + 1) * width]
 
-    @pl.loop(0, chunks)
-    def _(c):
-        for copy in in_copies(c):
-            copy.wait_send()
-        for copy in out_copies(c):
-            copy.wait()
-        for copy in own_outs(c):
-            copy.wait()
-
-    for copy in bias_col + mask_col + bias_row + part_row + part_col:
-        copy.wait_send()
+    ins = got.at[:, :, 0:others]
+    outs = stage.at[:, :, 0:others]
+    for ref, send in (
+        (ins, in_send), (outs, out_send), (first, bc_send), (most, br_send),
+        (many, pr_send), (few, pc_send),
+    ):
+        remote(ref, ref, send, send, near).wait_send()
+    remote(outs, outs, out_send, out_recv, near).wait_recv()
+
+
+def writer_kernel(*refs):
+    count = len(refs) // 2
+    sem = refs[-1]
+    copies = [
+        pltpu.make_async_copy(refs[n], refs[count + n], sem.at[n]) for n in range(count)
+    ]
+    for copy in copies:
+        copy.start()
+    for copy in copies:
+        copy.wait()
+
+
+def written(*arrays):
+    return pl.pallas_call(
+        writer_kernel,
+        name="write_grads",
+        out_shape=tuple(jax.ShapeDtypeStruct(a.shape, a.dtype) for a in arrays),
+        in_specs=[pl.BlockSpec(memory_space=pl.ANY)] * len(arrays),
+        out_specs=(pl.BlockSpec(memory_space=pl.ANY),) * len(arrays),
+        scratch_shapes=[pltpu.SemaphoreType.DMA((len(arrays),))],
+    )(*(pltpu.with_memory_space_constraint(a, pltpu.VMEM) for a in arrays))
 
 
 def fused(rows_n, cols_n, query_proj, key_proj, value_proj, pair_bias, pair_mask, grad_out):
@@ -436,8 +421,7 @@
     while pack * 2 <= HEADS and pack * 2 * width <= 128:
         pack = pack * 2
     packs = HEADS // pack
-    padded, lanes = round_up(keys, 16), round_up(pack * width, 128)
-    mask_lanes = round_up(rows, 128)
+    padded, lanes = round_up(keys + per, 16), round_up(pack * width, 128)
     chunk = 2 if per % 2 == 0 else 1
     chunks = per // chunk
     bf16, f32 = jnp.bfloat16, jnp.float32
@@ -445,39 +429,32 @@
     on_chip = pl.BlockSpec(memory_space=pltpu.VMEM)
     sem = pltpu.SemaphoreType.DMA
     tile_shape = pltpu.VMEM(query_proj.shape, bf16)
-    gq, gk, gv, gb = pl.pallas_call(
+    grads = pl.pallas_call(
         functools.partial(fused_kernel, rows_n, cols_n, pack),
         name="triangle_grads",
         out_shape=(
             tile_shape, tile_shape, tile_shape,
-            jax.ShapeDtypeStruct((HEADS, keys, width), f32),
+            pltpu.VMEM((HEADS, keys, width), f32),
         ),
         in_specs=[anywhere] * 4 + [on_chip] * 2,
         out_specs=(on_chip,) * 4,
         scratch_shapes=[
-            pltpu.VMEM((packs, padded, lanes), bf16),
-            pltpu.VMEM((width, mask_lanes), bf16),
+            pltpu.VMEM((cols_n, packs, padded, lanes), bf16),
             pltpu.VMEM((4, per, count, channels), bf16),
             pltpu.VMEM((3, per, count, channels), bf16),
             pltpu.VMEM((rows_n, cols_n, packs, padded, lanes), bf16),
-            pltpu.VMEM((count, mask_lanes), bf16),
+            pltpu.VMEM((count, padded - keys), f32),
             pltpu.VMEM((HEADS, count, count), f32),
             pltpu.VMEM((HEADS, count, count), f32),
             pltpu.VMEM((rows_n, HEADS, padded, count), bf16),
             pltpu.VMEM((rows_n, HEADS, padded, count), bf16),
             pltpu.VMEM((cols_n, packs, padded, lanes), bf16),
             pltpu.VMEM((cols_n, packs, padded, lanes), bf16),
-            sem((chunks, cols_n, 4)), sem((chunks, cols_n, 4)),
-            sem((chunks, cols_n, 3)), sem((chunks, cols_n, 3)),
-            sem((cols_n,)), sem((cols_n,)),
-            sem((rows_n,)), sem((rows_n,)),
-            sem((cols_n,)), sem((cols_n,)),
-            sem((rows_n,)), sem((rows_n,)),
-            sem((cols_n,)), sem((cols_n,)),
-            sem((6,)),
+            sem((chunks,)), sem((11,)), sem(()),
         ],
         compiler_params=pltpu.CompilerParams(collective_id=0, has_side_effects=True),
     )(query_proj, key_proj, value_proj, grad_out, jnp.transpose(pair_bias, (0, 2, 1)), pair_mask)
+    gq, gk, gv, gb = written(*grads)
     return gq, gk, gv, jnp.transpose(gb, (0, 2, 1))
 
 

time: 62.8 us -> 57.2 us (0.911)
  local copies, waits for them, and re-layouts: 2.85 us -> 0 us
  Pallas kernels: 59.1 us -> 56.3 us
    pallas_call x1, Pallas kernels: 59.1 us -> 55.3 us  [fused(): pl.pallas_call(functools.partial(fused_kernel, rows_n, cols_n, pack), nam...]
    unnamed x6 -> x0, local copies, waits for them, and re-layouts: 2.85 us -> none
    pallas_call x0 -> x1, Pallas kernels: none -> 0.95 us  [written(): pl.pallas_call(writer_kernel, name='write_grads', out_shape=tuple((jax.Sh...]
where the time goes in v1:
time: 57.2 us; the launch traced here: 56.9 us
  Pallas kernels  56.3 us (98%)
  between operations  0.64 us (1%)
    pallas_call x1, Pallas kernels, fused(): pl.pallas_call(functools.partial(fused_kernel, rows_n, cols_n, pack), nam...  55.3 us

profile of v1, /device:TPU:0, one launch (start us, length us, event | category | flops | bytes accessed | tf_op | source)
XLA Modules:
  0.0 56.9 jit_solution(13149537559837919824)
XLA Ops:
  0.6 55.3 %triangle_grads.1 = (bf16[24,48,128]{2,1,0:T(8,128)(2,1)S(1)}, bf16[24,48,128]{2,1,0:T(8,128)(2,1)S(1)}, bf16[24,48,128]{2,1,0:T(8,128)(2,1)S(1)}, f32[4,24,48]{2,1,0:T(8,128)S(1)}) custom-call(bf16[24,48,128]{2,1,0:T(8,128)(2,1)} %q_ref.1, bf16[24,48,128]{2,1,0:T(8,128)(2,1)} %k_ref.1, bf16[24,48,128]{2,1,0:T(8,128)(2,1)} %v_ref.1, ...), custom_call_target="tpu_custom_call" | custom-call | tf_op jit(solution)/shard_map/triangle_grads/pallas_call | solution.py:432
  56.0 0.9 %write_grads.1 = (bf16[24,48,128]{2,1,0:T(8,128)(2,1)}, bf16[24,48,128]{2,1,0:T(8,128)(2,1)}, bf16[24,48,128]{2,1,0:T(8,128)(2,1)}, f32[4,24,48]{2,1,0:T(8,128)}) custom-call(bf16[24,48,128]{2,1,0:T(8,128)(2,1)S(1)} %get-tuple-element.12.refs_0_, bf16[24,48,128]{2,1,0:T(8,128)(2,1)S(1)} %get-tuple-element.13.refs_1_, ...), custom_call_target="tpu_custom_call" | custom-call | tf_op jit(solution)/shard_map/write_grads/pallas_call | solution.py:406

commit v2 on v1

v2 whole, which is shorter than its diff:
```python
import functools
import math

import jax
import jax.numpy as jnp
from jax import lax
from jax.experimental import pallas as pl
from jax.experimental.pallas import tpu as pltpu
from jax.sharding import PartitionSpec as P

HEADS = 4
HEAD_DIM = 32


def block_grads(queries, keys_all, values_all, grads, mask_all, bias_full):
    block_rows, query_count, channel_count = queries.shape
    key_count = keys_all.shape[1]
    scale = 1.0 / math.sqrt(HEAD_DIM)
    query_heads = queries.reshape(block_rows, query_count, HEADS, HEAD_DIM)
    key_heads = keys_all.reshape(block_rows, key_count, HEADS, HEAD_DIM)
    value_heads = values_all.reshape(block_rows, key_count, HEADS, HEAD_DIM)
    grad_heads = grads.reshape(block_rows, query_count, HEADS, HEAD_DIM)
    masked = 1000000000.0 * (mask_all.astype(jnp.float32) - 1.0)
    scores = (
        jnp.einsum("bjhd,bkhd->bhjk", query_heads, key_heads, preferred_element_type=jnp.float32)
        * scale
    )
    scores = scores + bias_full.astype(jnp.float32)[None] + masked[:, None, None, :]
    top_score = jnp.max(scores, axis=-1, keepdims=True)
    weights = jnp.exp(scores - top_score)
    attn_probs = weights / jnp.sum(weights, axis=-1, keepdims=True)
    attn_low = attn_probs.astype(jnp.bfloat16)
    attended = jnp.einsum(
        "bhjk,bkhd->bjhd", attn_low, value_heads, preferred_element_type=jnp.float32
    )
    row_delta = jnp.sum(grad_heads.astype(jnp.float32) * attended, axis=-1)
    grad_probs = jnp.einsum(
        "bjhd,bkhd->bhjk", grad_heads, value_heads, preferred_element_type=jnp.float32
    )
    grad_scores = attn_probs * (grad_probs - jnp.transpose(row_delta, (0, 2, 1))[..., None])
    scores_low = grad_scores.astype(jnp.bfloat16)
    grad_queries = (
        jnp.einsum("bhjk,bkhd->bjhd", scores_low, key_heads, preferred_element_type=jnp.float32)
        * scale
    )
    grad_keys = (
        jnp.einsum("bhjk,bjhd->bkhd", scores_low, query_heads, preferred_element_type=jnp.float32)
        * scale
    )
    grad_values = jnp.einsum(
        "bhjk,bjhd->bkhd", attn_low, grad_heads, preferred_element_type=jnp.float32
    )
    bias_grad = jnp.sum(grad_scores, axis=0)
    return (
        grad_queries.reshape(block_rows, query_count, channel_count),
        grad_keys.reshape(block_rows, key_count, channel_count),
        grad_values.reshape(block_rows, key_count, channel_count),
        bias_grad,
    )


def all_blocks(queries, keys_all, values_all, grads, mask_all, bias_full):
    row_count, query_count, channel_count = queries.shape
    key_count = keys_all.shape[1]
    block_rows = 1
    while (
        block_rows * 2 <= row_count
        and row_count % (block_rows * 2) == 0
        and (block_rows * query_count < 512)
    ):
        block_rows = block_rows * 2
    steps_count = row_count // block_rows

    def split_rows(array):
        return array.reshape((steps_count, block_rows) + array.shape[1:])

    def one_block(bias_sum, pieces):
        grad_queries, grad_keys, grad_values, bias_grad = block_grads(
            pieces[0], pieces[1], pieces[2], pieces[3], pieces[4], bias_full
        )
        return (bias_sum + bias_grad, (grad_queries, grad_keys, grad_values))

    start_sum = jnp.zeros((HEADS, query_count, key_count), jnp.float32)
    bias_sum, stacked = lax.scan(
        one_block,
        start_sum,
        (
            split_rows(queries),
            split_rows(keys_all),
            split_rows(values_all),
            split_rows(grads),
            split_rows(mask_all),
        ),
    )
    return (
        stacked[0].reshape(row_count, query_count, channel_count),
        stacked[1].reshape(row_count, key_count, channel_count),
        stacked[2].reshape(row_count, key_count, channel_count),
        bias_sum,
    )


def local(query_proj, key_proj, value_proj, pair_bias, pair_mask, grad_out):
    bias_rows = lax.all_gather(pair_bias, "row", axis=2, tiled=True)
    mask_low = pair_mask.astype(jnp.bfloat16)
    local_tiles = (
        lax.all_to_all(query_proj, "col", split_axis=0, concat_axis=1, tiled=True),
        lax.all_to_all(key_proj, "col", split_axis=0, concat_axis=1, tiled=True),
        lax.all_to_all(value_proj, "col", split_axis=0, concat_axis=1, tiled=True),
        lax.all_to_all(grad_out, "col", split_axis=0, concat_axis=1, tiled=True),
        lax.all_to_all(mask_low, "col", split_axis=0, concat_axis=1, tiled=True),
    )
    bias_full = lax.all_gather(bias_rows, "col", axis=1, tiled=True)
    grad_queries, grad_keys, grad_values, bias_whole = all_blocks(
        local_tiles[0], local_tiles[1], local_tiles[2], local_tiles[3], local_tiles[4], bias_full
    )
    grad_query, grad_key, grad_value = (
        lax.all_to_all(
            grad_queries.astype(jnp.bfloat16), "col", split_axis=1, concat_axis=0, tiled=True
        ),
        lax.all_to_all(
            grad_keys.astype(jnp.bfloat16), "col", split_axis=1, concat_axis=0, tiled=True
        ),
        lax.all_to_all(
            grad_values.astype(jnp.bfloat16), "col", split_axis=1, concat_axis=0, tiled=True
        ),
    )
    bias_part = lax.psum_scatter(bias_whole, "col", scatter_dimension=1, tiled=True)
    grad_bias = lax.psum_scatter(bias_part, "row", scatter_dimension=2, tiled=True)
    return (grad_query, grad_key, grad_value, grad_bias)


MESH = pl.DeviceIdType.MESH


def round_up(value, step):
    return -(-value // step) * step


AHEAD = 3
OWN_AHEAD = 6
LAG = 5
QUERIES_FIRST = 5
OUT_FROM = 4


def split_kernel(
    rows_n, pack,
    q_ref, k_ref, v_ref, g_ref, bias_in, mask_in,
    gq_ref, gk_ref, gv_ref, gb_ref,
    bias_send, bias_got, bias_rows, bias_half, mask_send, mask_half, qg, kv, scores_at, probs_at,
    stats, stats_in, stage_q, stage_kv, stage_sum, gq_in, bias_sum, part, part_in, tile, tile_in,
    from_outer, keys_in, from_mate, stats_recv, gq_recv, own_recv, sems,
):
    row, col = lax.axis_index("row"), lax.axis_index("col")
    cols_n = 4
    rows, width, _ = q_ref.shape
    chunk = rows // from_outer.shape[0]
    chunks = rows // chunk
    half, count = 2 * width, cols_n * width
    upper = rows_n // 2
    keys = half // upper
    packs, padded, lanes = bias_send.shape
    scale = 1.0 / math.sqrt(HEAD_DIM)
    (own_sem, outer_send, mate_send, stats_send, gq_send, kv_send, kv_recv, mask_out, mask_got,
     bz_send, bz_recv, br_send, br_recv, pr_send, pr_recv, pc_send, pc_recv) = (
        sems.at[n] for n in range(17)
    )
    inner = (col == 1) | (col == 2)
    home = 1 + col // 2
    mate = 3 - col
    outer = 3 * (home - 1)
    bias_home = 1 + row // upper
    holder = col == bias_home
    slot = lax.rem(row, upper)
    local = lax.rem(col, 2) * width
    local_outer = width - local

    def at_block(position):
        return pl.ds(pl.multiple_of(position * width, width), width)

    def remote(src, dst, send, recv, peer):
        return pltpu.make_async_remote_copy(
            src_ref=src, dst_ref=dst, send_sem=send, recv_sem=recv,
            device_id=peer, device_id_type=MESH,
        )

    next_col = (row, lax.rem(col + 1, cols_n))

    def landed(ref, sem):
        remote(ref, ref, sem, sem, next_col).wait_recv()

    def left(ref, sem):
        remote(ref, ref, sem, sem, next_col).wait_send()

    nn = (((1,), (0,)), ((), ()))
    nt = (((1,), (1,)), ((), ()))
    tn = (((0,), (0,)), ((), ()))
    barrier = pltpu.get_barrier_semaphore()
    for d in range(1, cols_n):
        pl.semaphore_signal(
            barrier, inc=1, device_id=(row, lax.rem(col + d, cols_n)), device_id_type=MESH
        )
    for d in range(1, rows_n):
        pl.semaphore_signal(
            barrier, inc=1, device_id=(lax.rem(row + d, rows_n), col), device_id_type=MESH
        )
    my_block = at_block(col)
    mate_half = pl.ds(pl.multiple_of((2 - home) * half, half), half)

    @pl.when(inner)
    def _():
        for a, ref in enumerate((q_ref, g_ref)):
            pltpu.make_async_copy(ref, qg.at[a, :, my_block], own_sem).start()
        for a, ref in enumerate((k_ref, v_ref)):
            pltpu.make_async_copy(ref, kv.at[a, :, pl.ds(local, width)], own_sem).start()

    def shifted(shape, shift):
        at = lax.broadcasted_iota(jnp.int32, shape, 0)
        lane = lax.broadcasted_iota(jnp.int32, shape, 1)
        return jnp.where(lane == at + shift, 1.0, 0.0).astype(jnp.bfloat16)

    bias_send[...] = jnp.zeros_like(bias_send)
    for p in range(packs):
        flipped = jnp.zeros((keys, lanes), jnp.float32)
        for hh in range(pack):
            flipped = flipped + lax.dot_general(
                bias_in[p * pack + hh], shifted((width, lanes), hh * width), nn,
                preferred_element_type=jnp.float32,
            )
        bias_send[p, 0:keys, :] = flipped.astype(jnp.bfloat16)
    mask_send[...] = lax.dot_general(
        mask_in[...].astype(jnp.float32).astype(jnp.bfloat16),
        shifted((rows, mask_send.shape[1]), 0), tn, preferred_element_type=jnp.float32,
    ).astype(jnp.bfloat16)
    pl.semaphore_wait(barrier, rows_n + cols_n - 2)

    bias_piece = remote(
        bias_send, bias_got.at[col], bz_send, bz_recv, (row, bias_home)
    )

    @pl.when(jnp.logical_not(holder))
    def _():
        bias_piece.start()

    def rows_of(c):
        return pl.ds(c * chunk, chunk)

    @pl.when(jnp.logical_not(inner))
    def _():
        remote(
            mask_send, mask_half.at[pl.ds(local, width)], mask_out, mask_got, (row, home)
        ).start()

        def queries_start(c):
            for a, ref in enumerate((q_ref, g_ref)):
                remote(
                    ref.at[rows_of(c)], qg.at[a, rows_of(c), my_block],
                    outer_send, from_outer.at[c], (row, home),
                ).start()

        ahead = min(QUERIES_FIRST, chunks)
        pl.loop(0, ahead)(queries_start)

        @pl.loop(0, chunks)
        def _(c):
            for a, ref in enumerate((k_ref, v_ref)):
                remote(
                    ref.at[rows_of(c)], kv.at[a, rows_of(c), pl.ds(local, width)],
                    outer_send, keys_in.at[c], (row, home),
                ).start()

            @pl.when(c + ahead < chunks)
            def _():
                queries_start(c + ahead)

    def pick(z, hh, shape, lane_axis):
        lane = lax.broadcasted_iota(jnp.int32, shape, lane_axis)
        at = lax.broadcasted_iota(jnp.int32, shape, 1 - lane_axis)
        inside = (lane >= hh * width) & (lane < (hh + 1) * width)
        return jnp.where(inside & (lane + (z - hh) * width == at), 1.0, 0.0).astype(jnp.bfloat16)

    channel = lax.broadcasted_iota(jnp.int32, (1, HEADS * HEAD_DIM), 1)

    def only(x, h):
        mine = (channel >= h * HEAD_DIM) & (channel < (h + 1) * HEAD_DIM)
        return jnp.where(mine, x, jnp.zeros_like(x))

    def own_start(c):
        for a, ref in enumerate((q_ref, g_ref)):
            remote(
                ref.at[rows_of(c)], qg.at[a, rows_of(c), my_block],
                mate_send, from_mate.at[c], (row, mate),
            ).start()

    def relay(c):
        block = qg.at[:, rows_of(c), at_block(outer)]
        landed(block, from_outer.at[c])
        for a in range(2):
            block = qg.at[a, rows_of(c), at_block(outer)]
            remote(block, block, mate_send, from_mate.at[c], (row, mate)).start()

        @pl.when(c + OWN_AHEAD < chunks)
        def _():
            own_start(c + OWN_AHEAD)

    def first_pass(c):
        landed(qg.at[:, rows_of(c), mate_half], from_mate.at[c])
        landed(kv.at[:, rows_of(c), pl.ds(local_outer, width)], keys_in.at[c])
        there = lax.rem(c, LAG + 1)
        mask_lane = lax.broadcasted_iota(jnp.int32, mask_half.shape, 1)
        rows_stats = []
        for r in range(chunk):
            i = c * chunk + r
            q, g, k, v = qg[0, i], qg[1, i], kv[0, i], kv[1, i]
            present = jnp.sum(
                jnp.where(mask_lane == i, mask_half[...].astype(jnp.float32), 0.0),
                axis=1, keepdims=True,
            )
            masked = 1000000000.0 * (present - 1.0)
            some = jnp.max(present, axis=0, keepdims=True)
            shift = jnp.where(some > 0.0, 0.0, 1000000000.0 - 4096.0)
            stacked_keys = jnp.concatenate([only(k, h) for h in range(HEADS)], axis=0)
            stacked_values = jnp.concatenate([only(v, h) for h in range(HEADS)], axis=0)
            raw = lax.dot_general(stacked_keys, q, nt, preferred_element_type=jnp.float32)
            grad_probs = lax.dot_general(stacked_values, g, nt, preferred_element_type=jnp.float32)
            logs, deltas = [], []
            for h in range(HEADS):
                part_rows = slice(h * half, (h + 1) * half)
                score = raw[part_rows] * scale + bias_half[h]
                score = (score + masked) + shift
                grad_prob = grad_probs[part_rows]
                top = jnp.max(score, axis=0, keepdims=True)
                weights = jnp.exp(score - top)
                total = jnp.sum(weights, axis=0, keepdims=True)
                logs.append(top + jnp.log(total))
                deltas.append(jnp.sum(weights * grad_prob, axis=0, keepdims=True) / total)
                scores_at[there, r, h] = score
                probs_at[there, r, h] = grad_prob
            rows_stats.append(jnp.concatenate(logs + deltas, axis=0))
        stats[c] = jnp.concatenate(rows_stats, axis=1)
        remote(stats.at[c], stats_in.at[c], stats_send, stats_recv.at[c], (row, mate)).start()

    def second_pass(c):
        landed(stats_in.at[c], stats_recv.at[c])
        there = lax.rem(c, LAG + 1)
        here, other = stats[c], stats_in[c]
        log_here, log_other = here[0:HEADS], other[0:HEADS]
        top = jnp.maximum(log_here, log_other)
        log_all = top + jnp.log(jnp.exp(log_here - top) + jnp.exp(log_other - top))
        delta_all = (
            here[HEADS:2 * HEADS] * jnp.exp(log_here - log_all)
            + other[HEADS:2 * HEADS] * jnp.exp(log_other - log_all)
        )
        gqs = [jnp.zeros((count, HEADS * HEAD_DIM), jnp.float32)] * chunk
        gks = [jnp.zeros((half, HEADS * HEAD_DIM), jnp.float32)] * chunk
        gvs = list(gks)
        for h in range(HEADS):
            bias_part = bias_sum[h]
            for r in range(chunk):
                i = c * chunk + r
                lane_part = slice(r * count, (r + 1) * count)
                probs = jnp.exp(scores_at[there, r, h] - log_all[h:h + 1, lane_part])
                grad_scores = probs * (probs_at[there, r, h] - delta_all[h:h + 1, lane_part])
                bias_part = bias_part + grad_scores
                low, slow = probs.astype(jnp.bfloat16), grad_scores.astype(jnp.bfloat16)
                gqs[r] = gqs[r] + lax.dot_general(
                    slow, only(kv[0, i], h), tn, preferred_element_type=jnp.float32
                )
                gks[r] = gks[r] + jnp.dot(
                    slow, only(qg[0, i], h), preferred_element_type=jnp.float32
                )
                gvs[r] = gvs[r] + jnp.dot(
                    low, only(qg[1, i], h), preferred_element_type=jnp.float32
                )
            bias_sum[h] = bias_part
        for r in range(chunk):
            i = c * chunk + r
            stage_q[i] = (gqs[r] * scale).astype(jnp.bfloat16)
            stage_kv[0, i] = (gks[r] * scale).astype(jnp.bfloat16)
            stage_kv[1, i] = gvs[r].astype(jnp.bfloat16)
        for a, ref in enumerate((gk_ref, gv_ref)):
            remote(
                stage_kv.at[a, rows_of(c), pl.ds(local_outer, width)], ref.at[rows_of(c)],
                kv_send, kv_recv, (row, outer),
            ).start()
            ref[rows_of(c)] = stage_kv[a, rows_of(c), pl.ds(local, width)]

    groups = own_recv.shape[0]
    grouped = chunks // groups

    def outer_part(c):
        remote(
            stage_q.at[rows_of(c), at_block(3 - outer)], gq_in.at[rows_of(c), pl.ds(local, width)],
            gq_send, gq_recv.at[c], (row, mate),
        ).start()

    def own_rows(n):
        return pl.ds(n * grouped * chunk, grouped * chunk)

    def own_part(n):
        remote(
            stage_q.at[own_rows(n), at_block(mate)],
            gq_in.at[own_rows(n), pl.ds(local_outer, width)],
            gq_send, own_recv.at[n], (row, mate),
        ).start()

    def outer_sum(c):
        landed(gq_in.at[rows_of(c), pl.ds(local_outer, width)], gq_recv.at[c])
        total = stage_q[rows_of(c), at_block(outer)].astype(jnp.float32)
        total = total + gq_in[rows_of(c), pl.ds(local_outer, width)].astype(jnp.float32)
        stage_sum[rows_of(c)] = total.astype(jnp.bfloat16)
        remote(
            stage_sum.at[rows_of(c)], gq_ref.at[rows_of(c)], kv_send, kv_recv, (row, outer)
        ).start()

    @pl.when(inner)
    def _():
        for c in range(min(OWN_AHEAD, chunks)):
            own_start(c)
        bias_sum[...] = jnp.zeros_like(bias_sum)
        part[...] = jnp.zeros_like(part)
        mask_half[pl.ds(local, width)] = mask_send[...]

        @pl.when(holder)
        def _():
            bias_got[col] = bias_send[...]
            landed(bias_got.at[0:cols_n - 1], bz_recv)
            for p in range(packs):
                for hh in range(pack):
                    whole = jnp.zeros((padded, count), jnp.float32)
                    for z in range(cols_n):
                        whole = whole + jnp.dot(
                            bias_got[z, p], pick(z, hh, (lanes, count), 0),
                            preferred_element_type=jnp.float32,
                        )
                    bias_rows[slot, p * pack + hh] = whole.astype(jnp.bfloat16)
            for d in range(1, rows_n):
                remote(
                    bias_rows.at[slot], bias_rows.at[slot], br_send, br_recv,
                    (lax.rem(row + d, rows_n), col),
                ).start()

        pltpu.make_async_copy(
            qg.at[:, :, 0:half], qg.at[:, :, 0:half], own_sem
        ).wait()
        landed(mask_half.at[pl.ds(local_outer, width)], mask_got)

        @pl.loop(0, min(AHEAD, chunks))
        def _(c):
            relay(c)

        @pl.when(holder)
        def _():
            landed(bias_rows.at[0:upper - 1], br_recv)

        @pl.when(jnp.logical_not(holder))
        def _():
            landed(bias_rows, br_recv)

        for r in range(upper):
            for h in range(HEADS):
                bias_half[h, r * keys:(r + 1) * keys, :] = (
                    bias_rows[r, h].astype(jnp.float32)[0:keys]
                )

        out_from = max(chunks - OUT_FROM, LAG)
        own_steps = [
            max(out_from + 1 + 2 * n, (n + 1) * grouped - 1 + LAG) for n in range(groups)
        ]

        @pl.loop(0, chunks + LAG)
        def _(c):
            @pl.when(c + AHEAD < chunks)
            def _():
                relay(c + AHEAD)

            @pl.when(c < chunks)
            def _():
                first_pass(c)

            @pl.when(c >= LAG)
            def _():
                second_pass(c - LAG)

            @pl.when(c == out_from)
            def _():
                pl.loop(0, out_from - LAG)(outer_part)

            @pl.when(c >= out_from)
            def _():
                outer_part(c - LAG)

            for n in range(groups - 1):
                pl.when(c == own_steps[n])(functools.partial(own_part, n))

        own_part(groups - 1)

        for r in range(upper):
            for h in range(HEADS):
                part[r, h, 0:keys, :] = bias_sum[h, r * keys:(r + 1) * keys, :].astype(jnp.bfloat16)
        for r in range(upper):
            owner = (col - 1) * upper + r

            @pl.when(owner != row)
            def _():
                remote(part.at[r], part_in.at[row], pr_send, pr_recv, (owner, col)).start()

        pl.loop(0, chunks)(outer_sum)

        @pl.when(holder)
        def _():
            many = part_in.at[0:rows_n - 1]
            landed(many, pr_recv)
            sums = []
            for h in range(HEADS):
                total = part[slot, h].astype(jnp.float32)
                for d in range(1, rows_n):
                    total = total + part_in[lax.rem(row + d, rows_n), h].astype(jnp.float32)
                sums.append(total.astype(jnp.bfloat16))
            for z in range(cols_n):
                for p in range(packs):
                    packed = jnp.zeros((padded, lanes), jnp.float32)
                    for hh in range(pack):
                        packed = packed + jnp.dot(
                            sums[p * pack + hh], pick(z, hh, (count, lanes), 1),
                            preferred_element_type=jnp.float32,
                        )
                    tile[z, p] = packed.astype(jnp.bfloat16)
            for d in range(1, cols_n):
                there = lax.rem(col + d, cols_n)
                remote(tile.at[there], tile_in, pc_send, pc_recv, (row, there)).start()
            tile_in[...] = tile[col]
            left(many, br_send)
            left(part.at[0:upper - 1], pr_send)
            left(tile.at[0:cols_n - 1], pc_send)

        @pl.when(jnp.logical_not(holder))
        def _():
            left(part, pr_send)

        for n in range(groups):
            landed(gq_in.at[own_rows(n), pl.ds(local, width)], own_recv.at[n])

            @pl.loop(n * grouped, (n + 1) * grouped)
            def _(c):
                total = stage_q[rows_of(c), my_block].astype(jnp.float32)
                total = total + gq_in[rows_of(c), pl.ds(local, width)].astype(jnp.float32)
                gq_ref[rows_of(c)] = total.astype(jnp.bfloat16)

        left(qg.at[:, :, 0:half], mate_send)
        left(stats, stats_send)
        left(gq_in, gq_send)
        left(qg.at[0, :, 0:3 * width], kv_send)

    @pl.when(jnp.logical_not(inner))
    def _():
        landed(qg.at[0, :, 0:3 * width], kv_recv)
        left(mask_send, mask_out)
        left(qg.at[:, :, 0:half], outer_send)

    @pl.when(jnp.logical_not(holder))
    def _():
        landed(tile_in, pc_recv)
        bias_piece.wait_send()

    for p in range(packs):
        for hh in range(pack):
            gb_ref[p * pack + hh] = tile_in[
                p, 0:keys, hh * width:(hh + 1) * width
            ].astype(jnp.float32)


def writer_kernel(*refs):
    count = len(refs) // 2
    sem = refs[-1]
    copies = [
        pltpu.make_async_copy(refs[n], refs[count + n], sem.at[n]) for n in range(count)
    ]
    for copy in copies:
        copy.start()
    for copy in copies:
        copy.wait()


def written(*arrays):
    return pl.pallas_call(
        writer_kernel,
        name="write_grads",
        out_shape=tuple(jax.ShapeDtypeStruct(a.shape, a.dtype) for a in arrays),
        in_specs=[pl.BlockSpec(memory_space=pl.ANY)] * len(arrays),
        out_specs=(pl.BlockSpec(memory_space=pl.ANY),) * len(arrays),
        scratch_shapes=[pltpu.SemaphoreType.DMA((len(arrays),))],
    )(*(pltpu.with_memory_space_constraint(a, pltpu.VMEM) for a in arrays))


def fused(rows_n, query_proj, key_proj, value_proj, pair_bias, pair_mask, grad_out):
    rows, width, channels = query_proj.shape
    keys = pair_bias.shape[2]
    cols_n = 4
    half, count, upper = 2 * width, 4 * width, rows_n // 2
    pack = 1
    while pack * 2 <= HEADS and pack * 2 * width <= 128:
        pack = pack * 2
    packs = HEADS // pack
    padded, lanes = round_up(keys, 16), round_up(pack * width, 128)
    mask_lanes = round_up(rows, 128)
    chunk = 2 if rows % 2 == 0 else 1
    chunks = rows // chunk
    bf16, f32 = jnp.bfloat16, jnp.float32
    anywhere = pl.BlockSpec(memory_space=pl.ANY)
    on_chip = pl.BlockSpec(memory_space=pltpu.VMEM)
    sem = pltpu.SemaphoreType.DMA
    tile_shape = pltpu.VMEM(query_proj.shape, bf16)
    grads = pl.pallas_call(
        functools.partial(split_kernel, rows_n, pack),
        name="triangle_grads",
        out_shape=(
            tile_shape, tile_shape, tile_shape,
            pltpu.VMEM((HEADS, keys, width), f32),
        ),
        in_specs=[anywhere] * 4 + [on_chip] * 2,
        out_specs=(on_chip,) * 4,
        scratch_shapes=[
            pltpu.VMEM((packs, padded, lanes), bf16),
            pltpu.VMEM((cols_n, packs, padded, lanes), bf16),
            pltpu.VMEM((upper, HEADS, padded, count), bf16),
            pltpu.VMEM((HEADS, half, count), f32),
            pltpu.VMEM((width, mask_lanes), bf16),
            pltpu.VMEM((half, mask_lanes), bf16),
            pltpu.VMEM((2, rows, count, channels), bf16),
            pltpu.VMEM((2, rows, half, channels), bf16),
            pltpu.VMEM((LAG + 1, chunk, HEADS, half, count), f32),
            pltpu.VMEM((LAG + 1, chunk, HEADS, half, count), f32),
            pltpu.VMEM((chunks, 2 * HEADS, chunk * count), f32),
            pltpu.VMEM((chunks, 2 * HEADS, chunk * count), f32),
            pltpu.VMEM((rows, count, channels), bf16),
            pltpu.VMEM((2, rows, half, channels), bf16),
            pltpu.VMEM((rows, width, channels), bf16),
            pltpu.VMEM((rows, half, channels), bf16),
            pltpu.VMEM((HEADS, half, count), f32),
            pltpu.VMEM((upper, HEADS, padded, count), bf16),
            pltpu.VMEM((rows_n, HEADS, padded, count), bf16),
            pltpu.VMEM((cols_n, packs, padded, lanes), bf16),
            pltpu.VMEM((packs, padded, lanes), bf16),
            sem((chunks,)), sem((chunks,)), sem((chunks,)), sem((chunks,)), sem((chunks,)),
            sem((3 if chunks % 3 == 0 else 1,)), sem((17,)),
        ],
        compiler_params=pltpu.CompilerParams(collective_id=0, has_side_effects=True),
    )(query_proj, key_proj, value_proj, grad_out, jnp.transpose(pair_bias, (0, 2, 1)), pair_mask)
    gq, gk, gv, gb = written(*grads)
    return gq, gk, gv, jnp.transpose(gb, (0, 2, 1))


def choose(rows_n, cols_n):
    def run(*arrays):
        count = arrays[0].shape[1] * cols_n
        small = count * count * 4 <= 512 * 1024 and arrays[0].shape[0] <= 128
        if small and cols_n == 4 and rows_n % 2 == 0 and arrays[0].shape[1] % 16 == 0:
            return fused(rows_n, *arrays)
        return local(*arrays)

    return run


def solution(mesh):
    placed = (
        P("row", "col", None),
        P("row", "col", None),
        P("row", "col", None),
        P(None, "col", "row"),
        P("row", "col"),
        P("row", "col", None),
    )
    return jax.shard_map(
        choose(mesh.shape["row"], mesh.shape["col"]),
        mesh=mesh,
        in_specs=placed,
        out_specs=(
            P("row", "col", None),
            P("row", "col", None),
            P("row", "col", None),
            P(None, "col", "row"),
        ),
        check_vma=False,
    )
```

time: 57.2 us -> 55.1 us (0.963)
  Pallas kernels: 56.3 us -> 54.3 us
    pallas_call x1, Pallas kernels: 55.3 us -> 53.4 us  [fused(): pl.pallas_call(functools.partial(split_kernel, rows_n, pack), name='trian...]
where the time goes in v2:
time: 55.1 us; the launch traced here: 55 us
  Pallas kernels  54.3 us (99%)
  between operations  0.64 us (1%)
    pallas_call x1, Pallas kernels, fused(): pl.pallas_call(functools.partial(split_kernel, rows_n, pack), name='trian...  53.4 us

profile of v2, /device:TPU:0, one launch (start us, length us, event | category | flops | bytes accessed | tf_op | source)
XLA Modules:
  0.0 55.0 jit_solution(2902415648339569370)
XLA Ops:
  0.6 53.4 %triangle_grads.1 = (bf16[24,48,128]{2,1,0:T(8,128)(2,1)S(1)}, bf16[24,48,128]{2,1,0:T(8,128)(2,1)S(1)}, bf16[24,48,128]{2,1,0:T(8,128)(2,1)S(1)}, f32[4,24,48]{2,1,0:T(8,128)S(1)}) custom-call(bf16[24,48,128]{2,1,0:T(8,128)(2,1)} %q_ref.1, bf16[24,48,128]{2,1,0:T(8,128)(2,1)} %k_ref.1, bf16[24,48,128]{2,1,0:T(8,128)(2,1)} %v_ref.1, ...), custom_call_target="tpu_custom_call" | custom-call | tf_op jit(solution)/shard_map/triangle_grads/pallas_call | solution.py:615
  54.0 0.9 %write_grads.1 = (bf16[24,48,128]{2,1,0:T(8,128)(2,1)}, bf16[24,48,128]{2,1,0:T(8,128)(2,1)}, bf16[24,48,128]{2,1,0:T(8,128)(2,1)}, f32[4,24,48]{2,1,0:T(8,128)}) custom-call(bf16[24,48,128]{2,1,0:T(8,128)(2,1)S(1)} %get-tuple-element.12.refs_0_, bf16[24,48,128]{2,1,0:T(8,128)(2,1)S(1)} %get-tuple-element.13.refs_1_, ...), custom_call_target="tpu_custom_call" | custom-call | tf_op jit(solution)/shard_map/write_grads/pallas_call | solution.py:587

commit v3 on v2

--- a/solution.py
+++ b/solution.py
@@ -137,11 +137,14 @@
     return -(-value // step) * step
 
 
-AHEAD = 3
-OWN_AHEAD = 6
-LAG = 5
+AHEAD = 4
+OWN_AHEAD = 5
+LAG = 4
+LAST_SUMS = 1
 QUERIES_FIRST = 5
-OUT_FROM = 4
+FIRST_OUT = 5
+OUT_STEP = 4
+SUM_AFTER = 4
 
 
 def split_kernel(
@@ -149,8 +152,8 @@
     q_ref, k_ref, v_ref, g_ref, bias_in, mask_in,
     gq_ref, gk_ref, gv_ref, gb_ref,
     bias_send, bias_got, bias_rows, bias_half, mask_send, mask_half, qg, kv, scores_at, probs_at,
-    stats, stats_in, stage_q, stage_kv, stage_sum, gq_in, bias_sum, part, part_in, tile, tile_in,
-    from_outer, keys_in, from_mate, stats_recv, gq_recv, own_recv, sems,
+    logs_here, logs_other, deltas_here, deltas_other, both_stats, stage_q, stage_kv, stage_sum, gq_in, bias_sum, part, part_in, part_long, tile, tile_in,
+    from_outer, keys_in, from_mate, stats_recv, gq_recv, own_recv, sems, pc_recv, greets,
 ):
     row, col = lax.axis_index("row"), lax.axis_index("col")
     cols_n = 4
@@ -163,8 +166,8 @@
     packs, padded, lanes = bias_send.shape
     scale = 1.0 / math.sqrt(HEAD_DIM)
     (own_sem, outer_send, mate_send, stats_send, gq_send, kv_send, kv_recv, mask_out, mask_got,
-     bz_send, bz_recv, br_send, br_recv, pr_send, pr_recv, pc_send, pc_recv) = (
-        sems.at[n] for n in range(17)
+     bz_send, bz_recv, br_send, br_recv, pr_send, pr_recv, pc_send) = (
+        sems.at[n] for n in range(16)
     )
     inner = (col == 1) | (col == 2)
     home = 1 + col // 2
@@ -173,6 +176,9 @@
     bias_home = 1 + row // upper
     holder = col == bias_home
     slot = lax.rem(row, upper)
+    group = row // upper
+    owner = (col - 1) * upper + slot
+    bias_long = part_long.at[0:rows_n - 1]
     local = lax.rem(col, 2) * width
     local_outer = width - local
 
@@ -197,78 +203,88 @@
     nt = (((1,), (1,)), ((), ()))
     tn = (((0,), (0,)), ((), ()))
     barrier = pltpu.get_barrier_semaphore()
-    for d in range(1, cols_n):
-        pl.semaphore_signal(
-            barrier, inc=1, device_id=(row, lax.rem(col + d, cols_n)), device_id_type=MESH
-        )
-    for d in range(1, rows_n):
-        pl.semaphore_signal(
-            barrier, inc=1, device_id=(lax.rem(row + d, rows_n), col), device_id_type=MESH
-        )
+
+    def greet(sem, peer):
+        pl.semaphore_signal(sem, inc=1, device_id=peer, device_id_type=MESH)
+
+    beside = []
+    bit = 1
+    while bit < rows_n:
+        beside.append(row + bit - 2 * bit * lax.rem(row // bit, 2))
+        bit = bit * 2
+
+    @pl.when(inner)
+    def _():
+        greet(barrier, (row, mate))
+        for other in beside:
+            greet(barrier, (other, col))
+        greet(barrier, (row, outer))
+
     my_block = at_block(col)
     mate_half = pl.ds(pl.multiple_of((2 - home) * half, half), half)
-
-    @pl.when(inner)
-    def _():
-        for a, ref in enumerate((q_ref, g_ref)):
-            pltpu.make_async_copy(ref, qg.at[a, :, my_block], own_sem).start()
-        for a, ref in enumerate((k_ref, v_ref)):
-            pltpu.make_async_copy(ref, kv.at[a, :, pl.ds(local, width)], own_sem).start()
+    for a, ref in enumerate((q_ref, g_ref)):
+        pltpu.make_async_copy(ref, qg.at[a, :, my_block], own_sem).start()
+    for a, ref in enumerate((k_ref, v_ref)):
+        pltpu.make_async_copy(ref, kv.at[a, :, pl.ds(local, width)], own_sem).start()
+
+    def own_landed():
+        pltpu.make_async_copy(qg.at[:, :, 0:half], qg.at[:, :, 0:half], own_sem).wait()
 
     def shifted(shape, shift):
         at = lax.broadcasted_iota(jnp.int32, shape, 0)
         lane = lax.broadcasted_iota(jnp.int32, shape, 1)
         return jnp.where(lane == at + shift, 1.0, 0.0).astype(jnp.bfloat16)
 
-    bias_send[...] = jnp.zeros_like(bias_send)
-    for p in range(packs):
-        flipped = jnp.zeros((keys, lanes), jnp.float32)
-        for hh in range(pack):
-            flipped = flipped + lax.dot_general(
-                bias_in[p * pack + hh], shifted((width, lanes), hh * width), nn,
-                preferred_element_type=jnp.float32,
-            )
-        bias_send[p, 0:keys, :] = flipped.astype(jnp.bfloat16)
-    mask_send[...] = lax.dot_general(
-        mask_in[...].astype(jnp.float32).astype(jnp.bfloat16),
-        shifted((rows, mask_send.shape[1]), 0), tn, preferred_element_type=jnp.float32,
-    ).astype(jnp.bfloat16)
-    pl.semaphore_wait(barrier, rows_n + cols_n - 2)
+    def prepare():
+        bias_send[...] = jnp.zeros_like(bias_send)
+        for p in range(packs):
+            flipped = jnp.zeros((keys, lanes), jnp.float32)
+            for hh in range(pack):
+                flipped = flipped + lax.dot_general(
+                    bias_in[p * pack + hh], shifted((width, lanes), hh * width), nn,
+                    preferred_element_type=jnp.float32,
+                )
+            bias_send[p, 0:keys, :] = flipped.astype(jnp.bfloat16)
+        mask_send[...] = lax.dot_general(
+            mask_in[...].astype(jnp.float32).astype(jnp.bfloat16),
+            shifted((rows, mask_send.shape[1]), 0), tn, preferred_element_type=jnp.float32,
+        ).astype(jnp.bfloat16)
 
     bias_piece = remote(
         bias_send, bias_got.at[col], bz_send, bz_recv, (row, bias_home)
     )
 
-    @pl.when(jnp.logical_not(holder))
-    def _():
-        bias_piece.start()
-
     def rows_of(c):
         return pl.ds(c * chunk, chunk)
 
+    def queries_start(c):
+        for a in range(2):
+            block = qg.at[a, rows_of(c), my_block]
+            remote(block, block, outer_send, from_outer.at[c], (row, home)).start()
+
+    def keys_start(c):
+        for a in range(2):
+            block = kv.at[a, rows_of(c), pl.ds(local, width)]
+            remote(block, block, outer_send, keys_in.at[c], (row, home)).start()
+
     @pl.when(jnp.logical_not(inner))
     def _():
+        own_landed()
+        pl.semaphore_wait(barrier, 1)
+        ahead = min(QUERIES_FIRST, chunks)
+        pl.loop(0, min(2, ahead))(queries_start)
+        greet(greets.at[0], (row, home))
+        prepare()
         remote(
             mask_send, mask_half.at[pl.ds(local, width)], mask_out, mask_got, (row, home)
         ).start()
-
-        def queries_start(c):
-            for a, ref in enumerate((q_ref, g_ref)):
-                remote(
-                    ref.at[rows_of(c)], qg.at[a, rows_of(c), my_block],
-                    outer_send, from_outer.at[c], (row, home),
-                ).start()
-
-        ahead = min(QUERIES_FIRST, chunks)
-        pl.loop(0, ahead)(queries_start)
+        pl.semaphore_wait(barrier, 1)
+        bias_piece.start()
+        pl.loop(min(2, ahead), ahead)(queries_start)
 
         @pl.loop(0, chunks)
         def _(c):
-            for a, ref in enumerate((k_ref, v_ref)):
-                remote(
-                    ref.at[rows_of(c)], kv.at[a, rows_of(c), pl.ds(local, width)],
-                    outer_send, keys_in.at[c], (row, home),
-                ).start()
+            keys_start(c)
 
             @pl.when(c + ahead < chunks)
             def _():
@@ -287,11 +303,9 @@
         return jnp.where(mine, x, jnp.zeros_like(x))
 
     def own_start(c):
-        for a, ref in enumerate((q_ref, g_ref)):
-            remote(
-                ref.at[rows_of(c)], qg.at[a, rows_of(c), my_block],
-                mate_send, from_mate.at[c], (row, mate),
-            ).start()
+        for a in range(2):
+            block = qg.at[a, rows_of(c), my_block]
+            remote(block, block, mate_send, from_mate.at[c], (row, mate)).start()
 
     def relay(c):
         block = qg.at[:, rows_of(c), at_block(outer)]
@@ -309,7 +323,7 @@
         landed(kv.at[:, rows_of(c), pl.ds(local_outer, width)], keys_in.at[c])
         there = lax.rem(c, LAG + 1)
         mask_lane = lax.broadcasted_iota(jnp.int32, mask_half.shape, 1)
-        rows_stats = []
+        rows_logs, rows_deltas = [], []
         for r in range(chunk):
             i = c * chunk + r
             q, g, k, v = qg[0, i], qg[1, i], kv[0, i], kv[1, i]
@@ -337,20 +351,22 @@
                 deltas.append(jnp.sum(weights * grad_prob, axis=0, keepdims=True) / total)
                 scores_at[there, r, h] = score
                 probs_at[there, r, h] = grad_prob
-            rows_stats.append(jnp.concatenate(logs + deltas, axis=0))
-        stats[c] = jnp.concatenate(rows_stats, axis=1)
-        remote(stats.at[c], stats_in.at[c], stats_send, stats_recv.at[c], (row, mate)).start()
+            rows_logs.append(jnp.concatenate(logs, axis=0))
+            rows_deltas.append(jnp.concatenate(deltas, axis=0))
+        logs_here[c] = jnp.concatenate(rows_logs, axis=1)
+        deltas_here[c] = jnp.concatenate(rows_deltas, axis=1).astype(jnp.bfloat16)
+        for mine, theirs in ((logs_here, logs_other), (deltas_here, deltas_other)):
+            remote(mine.at[c], theirs.at[c], stats_send, stats_recv.at[c], (row, mate)).start()
 
     def second_pass(c):
-        landed(stats_in.at[c], stats_recv.at[c])
+        landed(both_stats.at[0], stats_recv.at[c])
         there = lax.rem(c, LAG + 1)
-        here, other = stats[c], stats_in[c]
-        log_here, log_other = here[0:HEADS], other[0:HEADS]
+        log_here, log_other = logs_here[c], logs_other[c]
         top = jnp.maximum(log_here, log_other)
         log_all = top + jnp.log(jnp.exp(log_here - top) + jnp.exp(log_other - top))
         delta_all = (
-            here[HEADS:2 * HEADS] * jnp.exp(log_here - log_all)
-            + other[HEADS:2 * HEADS] * jnp.exp(log_other - log_all)
+            deltas_here[c].astype(jnp.float32) * jnp.exp(log_here - log_all)
+            + deltas_other[c].astype(jnp.float32) * jnp.exp(log_other - log_all)
         )
         gqs = [jnp.zeros((count, HEADS * HEAD_DIM), jnp.float32)] * chunk
         gks = [jnp.zeros((half, HEADS * HEAD_DIM), jnp.float32)] * chunk
@@ -416,8 +432,23 @@
 
     @pl.when(inner)
     def _():
-        for c in range(min(OWN_AHEAD, chunks)):
-            own_start(c)
+        own_landed()
+        pl.semaphore_wait(barrier, 1 + len(beside))
+        greet(barrier, (row, outer))
+
+        own_first = min(OWN_AHEAD, chunks)
+        pl.loop(0, min(2, own_first))(own_start)
+        prepare()
+
+        @pl.when(jnp.logical_not(holder))
+        def _():
+            bias_piece.start()
+
+        pl.loop(min(2, own_first), own_first)(own_start)
+        for n in range(3, greets.shape[0]):
+            for other in beside:
+                greet(greets.at[n], (other, col))
+            pl.semaphore_wait(greets.at[n], len(beside))
         bias_sum[...] = jnp.zeros_like(bias_sum)
         part[...] = jnp.zeros_like(part)
         mask_half[pl.ds(local, width)] = mask_send[...]
@@ -441,9 +472,8 @@
                     (lax.rem(row + d, rows_n), col),
                 ).start()
 
-        pltpu.make_async_copy(
-            qg.at[:, :, 0:half], qg.at[:, :, 0:half], own_sem
-        ).wait()
+        pl.semaphore_wait(greets.at[0], 1)
+        greet(greets.at[1], (row, mate))
         landed(mask_half.at[pl.ds(local_outer, width)], mask_got)
 
         @pl.loop(0, min(AHEAD, chunks))
@@ -464,10 +494,9 @@
                     bias_rows[r, h].astype(jnp.float32)[0:keys]
                 )
 
-        out_from = max(chunks - OUT_FROM, LAG)
-        own_steps = [
-            max(out_from + 1 + 2 * n, (n + 1) * grouped - 1 + LAG) for n in range(groups)
-        ]
+        out_step = max(OUT_STEP, LAG)
+        first_out = max(min(FIRST_OUT, chunks - 1 - out_step), 0)
+        sum_step = min(out_step + SUM_AFTER, chunks + LAG - first_out)
 
         @pl.loop(0, chunks + LAG)
         def _(c):
@@ -483,61 +512,70 @@
             def _():
                 second_pass(c - LAG)
 
-            @pl.when(c == out_from)
-            def _():
-                pl.loop(0, out_from - LAG)(outer_part)
-
-            @pl.when(c >= out_from)
+            @pl.when((c >= out_step) & (c < out_step + first_out))
+            def _():
+                outer_part(c - out_step)
+
+            @pl.when(c == chunks - 1)
+            def _():
+                pl.loop(first_out, max(chunks - LAG, 0))(outer_part)
+
+            @pl.when(c >= max(chunks, LAG))
             def _():
                 outer_part(c - LAG)
 
-            for n in range(groups - 1):
-                pl.when(c == own_steps[n])(functools.partial(own_part, n))
-
-        own_part(groups - 1)
+            @pl.when((c >= sum_step) & (c < sum_step + first_out))
+            def _():
+                outer_sum(c - sum_step)
 
         for r in range(upper):
             for h in range(HEADS):
-                part[r, h, 0:keys, :] = bias_sum[h, r * keys:(r + 1) * keys, :].astype(jnp.bfloat16)
-        for r in range(upper):
-            owner = (col - 1) * upper + r
-
-            @pl.when(owner != row)
-            def _():
-                remote(part.at[r], part_in.at[row], pr_send, pr_recv, (owner, col)).start()
-
-        pl.loop(0, chunks)(outer_sum)
-
-        @pl.when(holder)
-        def _():
-            many = part_in.at[0:rows_n - 1]
-            landed(many, pr_recv)
-            sums = []
-            for h in range(HEADS):
-                total = part[slot, h].astype(jnp.float32)
-                for d in range(1, rows_n):
-                    total = total + part_in[lax.rem(row + d, rows_n), h].astype(jnp.float32)
-                sums.append(total.astype(jnp.bfloat16))
-            for z in range(cols_n):
-                for p in range(packs):
-                    packed = jnp.zeros((padded, lanes), jnp.float32)
-                    for hh in range(pack):
-                        packed = packed + jnp.dot(
-                            sums[p * pack + hh], pick(z, hh, (count, lanes), 1),
-                            preferred_element_type=jnp.float32,
-                        )
-                    tile[z, p] = packed.astype(jnp.bfloat16)
-            for d in range(1, cols_n):
-                there = lax.rem(col + d, cols_n)
-                remote(tile.at[there], tile_in, pc_send, pc_recv, (row, there)).start()
-            tile_in[...] = tile[col]
-            left(many, br_send)
-            left(part.at[0:upper - 1], pr_send)
-            left(tile.at[0:cols_n - 1], pc_send)
-
-        @pl.when(jnp.logical_not(holder))
-        def _():
-            left(part, pr_send)
+                part[h // pack, r, h % pack, 0:keys, :] = (
+                    bias_sum[h, r * keys:(r + 1) * keys, :].astype(jnp.bfloat16)
+                )
+        for d in range(1, rows_n):
+            peer = lax.rem(row + d, rows_n)
+            remote(
+                part.at[peer // upper, lax.rem(peer, upper)], part_in.at[row],
+                pr_send, pr_recv, (peer, col),
+            ).start()
+        for n in range(groups):
+            own_part(n)
+        last_sums = max(chunks - LAST_SUMS, first_out)
+        pl.loop(first_out, last_sums)(outer_sum)
+        pl.semaphore_wait(greets.at[1], 1)
+        greet(greets.at[2], (lax.rem(row + upper, rows_n), col))
+        pl.semaphore_wait(greets.at[2], 1)
+
+        many = part_in.at[0:rows_n - 1]
+        landed(many, pr_recv)
+        sums = []
+        for hh in range(pack):
+            total = part[group, slot, hh].astype(jnp.float32)
+            for d in range(1, rows_n):
+                total = total + part_in[lax.rem(row + d, rows_n), hh].astype(jnp.float32)
+            sums.append(total.astype(jnp.bfloat16))
+        for z in range(cols_n):
+            packed = jnp.zeros((padded, lanes), jnp.float32)
+            for hh in range(pack):
+                packed = packed + jnp.dot(
+                    sums[hh], pick(z, hh, (count, lanes), 1), preferred_element_type=jnp.float32
+                )
+            tile[z] = packed.astype(jnp.bfloat16)
+        for z in range(cols_n):
+            elsewhere = (owner != row) | (col != z)
+
+            @pl.when(elsewhere)
+            def _():
+                remote(
+                    tile.at[z], tile_in.at[group], pc_send, pc_recv.at[group], (owner, z)
+                ).start()
+
+        @pl.when(owner == row)
+        def _():
+            tile_in[group] = tile[col]
+
+        pl.loop(last_sums, chunks)(outer_sum)
 
         for n in range(groups):
             landed(gq_in.at[own_rows(n), pl.ds(local, width)], own_recv.at[n])
@@ -548,8 +586,19 @@
                 total = total + gq_in[rows_of(c), pl.ds(local, width)].astype(jnp.float32)
                 gq_ref[rows_of(c)] = total.astype(jnp.bfloat16)
 
+        left(part_in.at[0:rows_n - 1], pr_send)
+
+        @pl.when(holder)
+        def _():
+            left(bias_long, br_send)
+            left(tile.at[0:cols_n - 1], pc_send)
+
+        @pl.when(jnp.logical_not(holder))
+        def _():
+            left(tile, pc_send)
+
         left(qg.at[:, :, 0:half], mate_send)
-        left(stats, stats_send)
+        left(both_stats, stats_send)
         left(gq_in, gq_send)
         left(qg.at[0, :, 0:3 * width], kv_send)
 
@@ -559,9 +608,13 @@
         left(mask_send, mask_out)
         left(qg.at[:, :, 0:half], outer_send)
 
+    for n in range(packs):
+        @pl.when(jnp.logical_not(holder & (group == n)))
+        def _():
+            landed(tile_in.at[n], pc_recv.at[n])
+
     @pl.when(jnp.logical_not(holder))
     def _():
-        landed(tile_in, pc_recv)
         bias_piece.wait_send()
 
     for p in range(packs):
@@ -632,19 +685,23 @@
             pltpu.VMEM((2, rows, half, channels), bf16),
             pltpu.VMEM((LAG + 1, chunk, HEADS, half, count), f32),
             pltpu.VMEM((LAG + 1, chunk, HEADS, half, count), f32),
-            pltpu.VMEM((chunks, 2 * HEADS, chunk * count), f32),
-            pltpu.VMEM((chunks, 2 * HEADS, chunk * count), f32),
+            pltpu.VMEM((chunks, HEADS, chunk * count), f32),
+            pltpu.VMEM((chunks, HEADS, chunk * count), f32),
+            pltpu.VMEM((chunks, HEADS, chunk * count), bf16),
+            pltpu.VMEM((chunks, HEADS, chunk * count), bf16),
+            pltpu.VMEM((chunks, 3, HEADS, chunk * count), bf16),
             pltpu.VMEM((rows, count, channels), bf16),
             pltpu.VMEM((2, rows, half, channels), bf16),
             pltpu.VMEM((rows, width, channels), bf16),
             pltpu.VMEM((rows, half, channels), bf16),
             pltpu.VMEM((HEADS, half, count), f32),
-            pltpu.VMEM((upper, HEADS, padded, count), bf16),
+            pltpu.VMEM((packs, upper, pack, padded, count), bf16),
+            pltpu.VMEM((rows_n, pack, padded, count), bf16),
             pltpu.VMEM((rows_n, HEADS, padded, count), bf16),
-            pltpu.VMEM((cols_n, packs, padded, lanes), bf16),
+            pltpu.VMEM((cols_n, padded, lanes), bf16),
             pltpu.VMEM((packs, padded, lanes), bf16),
             sem((chunks,)), sem((chunks,)), sem((chunks,)), sem((chunks,)), sem((chunks,)),
-            sem((3 if chunks % 3 == 0 else 1,)), sem((17,)),
+            sem((3 if chunks % 3 == 0 else 1,)), sem((16,)), sem((packs,)), pltpu.SemaphoreType.REGULAR((rows_n.bit_length() + 1,)),
         ],
         compiler_params=pltpu.CompilerParams(collective_id=0, has_side_effects=True),
     )(query_proj, key_proj, value_proj, grad_out, jnp.transpose(pair_bias, (0, 2, 1)), pair_mask)
@@ -656,7 +713,9 @@
     def run(*arrays):
         count = arrays[0].shape[1] * cols_n
         small = count * count * 4 <= 512 * 1024 and arrays[0].shape[0] <= 128
-        if small and cols_n == 4 and rows_n % 2 == 0 and arrays[0].shape[1] % 16 == 0:
+        width = arrays[0].shape[1]
+        paired = HEADS == 4 and 32 < width <= 64 and rows_n > 1 and rows_n & (rows_n - 1) == 0
+        if small and cols_n == 4 and paired and width % 16 == 0:
             return fused(rows_n, *arrays)
         return local(*arrays)
 

time: 55.1 us -> 51.3 us (0.931)
  Pallas kernels: 54.3 us -> 50.5 us
    pallas_call x1, Pallas kernels: 53.4 us -> 49.5 us  [fused(): pl.pallas_call(functools.partial(split_kernel, rows_n, pack), name='trian...]
where the time goes in v3:
time: 51.3 us; the launch traced here: 51.1 us
  Pallas kernels  50.5 us (98%)
  between operations  0.64 us (1%)
    pallas_call x1, Pallas kernels, fused(): pl.pallas_call(functools.partial(split_kernel, rows_n, pack), name='trian...  49.5 us

profile of v3, /device:TPU:0, one launch (start us, length us, event | category | flops | bytes accessed | tf_op | source)
XLA Modules:
  0.0 51.1 jit_solution(10722040402978316254)
XLA Ops:
  0.6 49.5 %triangle_grads.1 = (bf16[24,48,128]{2,1,0:T(8,128)(2,1)S(1)}, bf16[24,48,128]{2,1,0:T(8,128)(2,1)S(1)}, bf16[24,48,128]{2,1,0:T(8,128)(2,1)S(1)}, f32[4,24,48]{2,1,0:T(8,128)S(1)}) custom-call(bf16[24,48,128]{2,1,0:T(8,128)(2,1)} %q_ref.1, bf16[24,48,128]{2,1,0:T(8,128)(2,1)} %k_ref.1, bf16[24,48,128]{2,1,0:T(8,128)(2,1)} %v_ref.1, ...), custom_call_target="tpu_custom_call" | custom-call | tf_op jit(solution)/shard_map/triangle_grads/pallas_call | solution.py:668
  50.1 0.9 %write_grads.1 = (bf16[24,48,128]{2,1,0:T(8,128)(2,1)}, bf16[24,48,128]{2,1,0:T(8,128)(2,1)}, bf16[24,48,128]{2,1,0:T(8,128)(2,1)}, f32[4,24,48]{2,1,0:T(8,128)}) custom-call(bf16[24,48,128]{2,1,0:T(8,128)(2,1)S(1)} %get-tuple-element.12.refs_0_, bf16[24,48,128]{2,1,0:T(8,128)(2,1)S(1)} %get-tuple-element.13.refs_1_, ...), custom_call_target="tpu_custom_call" | custom-call | tf_op jit(solution)/shard_map/write_grads/pallas_call | solution.py:640
